TPU v7x, 32 devices: a whole 2x2x4 slice. The times are simulated.
32 devices in a mesh: boxes: 32 (over z, y, x, core).
Axes of the slice: x: 2, y: 2, z: 4, core: 2. Of those that a mesh axis runs over, the one named last changes fastest.
Arguments:
- conserved: float32 [32, 5, 16, 32, 128], P('boxes'), may hold values from -6 to 6
- volume_fraction: float32 [32, 16, 32, 128], P('boxes'), may hold values from 0.05 to 1
- cut_mask: int32 [32, 16, 32, 128], P('boxes'), may hold values 0 or 1
- merge_code: int32 [32, 16, 32, 128], P('boxes'), may hold values from 0 to 26
Outputs:
- redistributed: float32 [32, 5, 16, 32, 128], P('boxes')
All inputs are finite; a program needn't handle non-finite values. No bound on the sum of `cut_mask` on one device may be relied on, other than what follows from the above.
Results may differ from a plain program's by a relative error of at most 0.0003.
Values sent between devices are 32-bit elements; how exact they have to be, the bound alone decides.
A program may use at most 64 MiB of HBM per device.

v0:
```python
import jax
import jax.numpy as jnp
from jax import lax
from jax.sharding import PartitionSpec as P

NBY = 4
NBZ = 4


OFFSETS = [
    (first, second, third)
    for first in (-1, 0, 1)
    for second in (-1, 0, 1)
    for third in (-1, 0, 1)
    if (first, second, third) != (0, 0, 0)
]


def shifted(shard, axis, by):
    devices = lax.axis_size(axis)
    pairs = [(i, i + by) for i in range(devices) if 0 <= i + by < devices]
    return lax.ppermute(shard, axis, pairs)


def decode(code_field):
    sign_parts = (code_field // 9 - 1, code_field // 3 % 3 - 1, code_field % 3 - 1)
    members = []
    for offset in OFFSETS:
        inside = jnp.ones(code_field.shape, jnp.bool_)
        for direction, component in zip(sign_parts, offset):
            if component != 0:
                inside = inside & (direction == component)
        members.append(inside)
    return members


def placed(values, offset):
    spread = [(0, 0)] * (values.ndim - 3) + [(1 + component, 1 - component) for component in offset]
    return jnp.pad(values, spread)


def count_members(members):
    running = placed(jnp.ones(members[0].shape, jnp.float32), (0, 0, 0))
    for offset, inside in zip(OFFSETS, members):
        running = running + placed(inside.astype(jnp.float32), offset)
    return running


def window(weighted, offset, interior):
    starts = [0] + [1 + component for component in offset]
    limits = [weighted.shape[0]] + [anchor + extent for anchor, extent in zip(starts[1:], interior)]
    return lax.slice(weighted, starts, limits)


def neighbour_average(weighted, members):
    interior = [extent - 2 for extent in weighted.shape[1:]]
    running = window(weighted, (0, 0, 0), interior)
    for offset, inside in zip(OFFSETS, members):
        running = running + jnp.where(inside[None], window(weighted, offset, interior), 0.0)
    return running[1:] / running[0:1]


def spread_back(average, members):
    running = placed(average, (0, 0, 0))
    for offset, inside in zip(OFFSETS, members):
        running = running + placed(jnp.where(inside[None], average, 0.0), offset)
    return running


def exchange_rims(values, spatial_dim, stride, layers, low_edge, high_edge):
    extent = values.shape[spatial_dim]
    lower_rim = lax.slice_in_dim(values, 0, layers, axis=spatial_dim)
    upper_rim = lax.slice_in_dim(values, extent - layers, extent, axis=spatial_dim)
    from_below = shifted(upper_rim, "boxes", stride)
    from_above = shifted(lower_rim, "boxes", -stride)
    from_below = jnp.where(low_edge, 0.0, from_below)
    from_above = jnp.where(high_edge, 0.0, from_above)
    return jnp.concatenate([from_below, values, from_above], axis=spatial_dim)


def fill_ghosts(values, layers, edges):
    strides = (NBY * NBZ, NBZ, 1)
    for spatial_dim in (3, 2, 1):
        low_edge, high_edge = edges[spatial_dim - 1]
        values = exchange_rims(
            values, spatial_dim, strides[spatial_dim - 1], layers, low_edge, high_edge
        )
    return values


def return_rims(values, spatial_dim, stride, low_edge, high_edge):
    extent = values.shape[spatial_dim]
    lower_ghost = lax.slice_in_dim(values, 0, 1, axis=spatial_dim)
    upper_ghost = lax.slice_in_dim(values, extent - 1, extent, axis=spatial_dim)
    from_below = shifted(upper_ghost, "boxes", stride)
    from_above = shifted(lower_ghost, "boxes", -stride)
    from_below = jnp.where(low_edge, 0.0, from_below)
    from_above = jnp.where(high_edge, 0.0, from_above)
    leading = lax.slice_in_dim(values, 1, 2, axis=spatial_dim) + from_below
    middle = lax.slice_in_dim(values, 2, extent - 2, axis=spatial_dim)
    trailing = lax.slice_in_dim(values, extent - 2, extent - 1, axis=spatial_dim) + from_above
    return jnp.concatenate([leading, middle, trailing], axis=spatial_dim)


def sum_ghosts(values, edges):
    strides = (NBY * NBZ, NBZ, 1)
    for spatial_dim in (1, 2, 3):
        low_edge, high_edge = edges[spatial_dim - 1]
        values = return_rims(values, spatial_dim, strides[spatial_dim - 1], low_edge, high_edge)
    return values


def per_device(conserved, volume_fraction, cut_mask, merge_code):
    fields = conserved[0]
    fraction = volume_fraction[0]
    code_field = jnp.where(cut_mask[0] == 1, merge_code[0], 13)
    position = lax.axis_index("boxes")
    box_x = position // (NBY * NBZ)
    box_y = position // NBZ % NBY
    box_z = position % NBZ
    edges = (
        (box_x == 0, box_x == lax.axis_size("boxes") // (NBY * NBZ) - 1),
        (box_y == 0, box_y == NBY - 1),
        (box_z == 0, box_z == NBZ - 1),
    )
    members = decode(code_field)
    counts_ghost = count_members(members)[None]
    counts = sum_ghosts(counts_ghost, edges)[0]
    weight = fraction / counts
    packed = jnp.concatenate([weight[None], weight[None] * fields], axis=0)
    weighted = fill_ghosts(packed, 1, edges)
    average = neighbour_average(weighted, members)
    deposits = spread_back(average, members)
    gathered = sum_ghosts(deposits, edges)
    return (gathered / counts[None])[None]


def solution(mesh):
    return jax.shard_map(
        per_device,
        mesh=mesh,
        in_specs=(
            P("boxes", None, None, None, None),
            P("boxes", None, None, None),
            P("boxes", None, None, None),
            P("boxes", None, None, None),
        ),
        out_specs=P("boxes", None, None, None, None),
        check_vma=False,
    )
```

profile of v0, /device:TPU:5, one launch (start us, length us, event | category | flops | bytes accessed | tf_op | source)
XLA Modules:
  0.0 217.8 jit_solution(16279148314739238653)
XLA Ops:
  0.0 2.5 %and_bitcast_fusion.15 = (pred[16,32,128]{2,0,1:T(8,128)(4,1)}, pred[1,16,32,128]{3,1,2,0:T(8,128)(4,1)S(1)}, pred[1,16,32,128]{3,1,2,0:T(8,128)(4,1)S(1)}, pred...) fusion(s32[1,16,32,128]{3,2,1,0:T(8,128)} %param.7, ...), kind=kLoop, calls=%fused_computation.153 | loop fusion | flops 2228224 | bytes 1441792 | tf_op jit(solution)/shard_map/jit(_where)/broadcast_in_dim | solution.py:59
  4.2 3.8 %add_bitcast_fusion = f32[1,18,34,130]{3,1,2,0:T(8,128)S(1)} fusion(f32[16,32,128]{2,0,1:T(8,128)S(1)} %broadcast_in_dim.486, pred[16,32,128]{2,0,1:T(8,128)(4,1)S(1)} %and.272, pred[16,32,128]{2,0,1:T(8,128)(4,1)S(1)} %get-tuple-element.36, pred[16,32,128]{2,0,1:T(8,128)(4,1)S(1)} %get-tuple-element.35, pred[16,32,128]{2,0,1:T(8,128)(4,1)S(1)} %get-tuple-element.113, ...), kind=kLoop, calls=%fused_computation.74 | loop fusion | flops 4137120 | bytes 2284320 | tf_op jit(solution)/shard_map/broadcast_in_dim | solution.py:127
  8.0 4.2 %collective-permute-start = (f32[1,1,34,130]{3,1,2,0:T(1,128)S(1)}, f32[1,1,34,130]{3,1,2,0:T(1,128)S(1)}, u32[]{:S(2)}, u32[]{:S(2)}) collective-permute-start(f32[1,1,34,130]{3,1,2,0:T(1,128)S(1)} %slice.283), channel_id=1, source_target_pairs={{0,16},{1,17},{2,18},{3,19},{4,20},{5,21},{6,22},{7,23},{8,24},{9,... | collective-permute-start | bytes 53048 | tf_op jit(solution)/shard_map/ppermute | solution.py:22
  14.7 4.2 %collective-permute-done.1 = f32[1,1,34,130]{3,1,2,0:T(1,128)S(1)} collective-permute-done((f32[1,1,34,130]{3,1,2,0:T(1,128)S(1)}, f32[1,1,34,130]{3,1,2,0:T(1,128)S(1)}, u32[]{:S(2)}, u32[]{:S(2)}) %collective-permute-start.1) | collective-permute-done | bytes 17712 | tf_op jit(solution)/shard_map/ppermute | solution.py:22
  19.0 3.2 %collective-permute-start.2 = (f32[1,16,1,130]{3,1,2,0:T(8,128)S(1)}, f32[1,16,1,130]{3,1,2,0:T(8,128)S(1)}, u32[]{:S(2)}, u32[]{:S(2)}) collective-permute-start(f32[1,16,1,130]{3,1,2,0:T(8,128)S(1)} %pad_maximum_fusion.21), channel_id=1, source_target_pairs={{0,4},{1,5},{2,6},{3,7},{4,8},{5,9},{6,10},{7,11},{8,12},{9,13},{1... | collective-permute-start | bytes 24968 | tf_op jit(solution)/shard_map/ppermute | solution.py:22
  25.9 3.0 %collective-permute-done.3 = f32[1,16,1,130]{3,1,2,0:T(8,128)S(1)} collective-permute-done((f32[1,16,1,130]{3,1,2,0:T(8,128)S(1)}, f32[1,16,1,130]{3,1,2,0:T(8,128)S(1)}, u32[]{:S(2)}, u32[]{:S(2)}) %collective-permute-start.3) | collective-permute-done | bytes 8352 | tf_op jit(solution)/shard_map/ppermute | solution.py:22
  29.2 8.0 %collective-permute-start.4 = (f32[1,16,32,1]{3,2,1,0:T(8,128)S(1)}, f32[1,16,32,1]{3,2,1,0:T(8,128)S(1)}, u32[]{:S(2)}, u32[]{:S(2)}) collective-permute-start(f32[1,16,32,1]{3,2,1,0:T(8,128)S(1)} %slice.289), channel_id=1, source_target_pairs={{0,1},{1,2},{2,3},{3,4},{4,5},{5,6},{6,7},{7,8},{8,9},{9,10},{10,1... | collective-permute-start | bytes 6152 | tf_op jit(solution)/shard_map/ppermute | solution.py:22
  37.2 3.3 %collective-permute-done.4 = f32[1,16,32,1]{3,2,1,0:T(8,128)S(1)} collective-permute-done((f32[1,16,32,1]{3,2,1,0:T(8,128)S(1)}, f32[1,16,32,1]{3,2,1,0:T(8,128)S(1)}, u32[]{:S(2)}, u32[]{:S(2)}) %collective-permute-start.4) | collective-permute-done | bytes 2080 | tf_op jit(solution)/shard_map/ppermute | solution.py:22
  40.6 4.2 %collective-permute-start.5 = (f32[1,16,32,1]{3,2,1,0:T(8,128)S(1)}, f32[1,16,32,1]{3,2,1,0:T(8,128)S(1)}, u32[]{:S(2)}, u32[]{:S(2)}) collective-permute-start(f32[1,16,32,1]{3,2,1,0:T(8,128)S(1)} %get-tuple-element.85), channel_id=1, source_target_pairs={{1,0},{2,1},{3,2},{4,3},{5,4},{6,5},{7,6},{8,7},{9,8},{10,9},{11,1... | collective-permute-start | bytes 6152 | tf_op jit(solution)/shard_map/ppermute | solution.py:22
  46.2 2.8 %collective-permute-done.5 = f32[1,16,32,1]{3,2,1,0:T(8,128)S(1)} collective-permute-done((f32[1,16,32,1]{3,2,1,0:T(8,128)S(1)}, f32[1,16,32,1]{3,2,1,0:T(8,128)S(1)}, u32[]{:S(2)}, u32[]{:S(2)}) %collective-permute-start.5) | collective-permute-done | bytes 2080 | tf_op jit(solution)/shard_map/ppermute | solution.py:22
  52.9 2.6 %copy.352 = f32[6,16,32,1]{2,1,3,0:T(8,128)} copy(f32[6,16,32,1]{3,2,1,0:T(8,128)} %get-tuple-element.51) | data formatting | bytes 24576
  59.8 2.4 %collective-permute-start.7 = (f32[6,16,32,1]{2,1,3,0:T(8,128)}, f32[6,16,32,1]{2,1,3,0:T(8,128)}, u32[]{:S(2)}, u32[]{:S(2)}) collective-permute-start(f32[6,16,32,1]{2,1,3,0:T(8,128)} %copy.353), channel_id=1, source_target_pairs={{1,0},{2,1},{3,2},{4,3},{5,4},{6,5},{7,6},{8,7},{9,8},{10,9},{11,1... | collective-permute-start | bytes 36872 | tf_op jit(solution)/shard_map/ppermute | solution.py:22
  62.2 2.6 %copy.332 = f32[6,16,32,1]{3,1,2,0:T(8,128)} copy(f32[6,16,32,1]{2,1,3,0:T(8,128)} %collective-permute-done.6) | data formatting | bytes 24576 | tf_op jit(solution)/shard_map/ppermute | solution.py:22
  67.3 2.6 %copy.334 = f32[6,16,32,1]{3,1,2,0:T(8,128)} copy(f32[6,16,32,1]{2,1,3,0:T(8,128)} %collective-permute-done.7) | data formatting | bytes 24576 | tf_op jit(solution)/shard_map/ppermute | solution.py:22
  71.6 2.5 %collective-permute-start.8 = (f32[6,16,1,130]{3,1,2,0:T(8,128)S(1)}, f32[6,16,1,130]{3,1,2,0:T(8,128)S(1)}, u32[]{:S(2)}, u32[]{:S(2)}) collective-permute-start(f32[6,16,1,130]{3,1,2,0:T(8,128)S(1)} %get-tuple-element.43), channel_id=1, source_target_pairs={{0,4},{1,5},{2,6},{3,7},{4,8},{5,9},{6,10},{7,11},{8,12},{9,13},{1... | collective-permute-start | bytes 149768 | tf_op jit(solution)/shard_map/ppermute | solution.py:22
  75.5 3.0 %collective-permute-start.9 = (f32[6,16,1,130]{3,1,2,0:T(8,128)S(1)}, f32[6,16,1,130]{3,1,2,0:T(8,128)S(1)}, u32[]{:S(2)}, u32[]{:S(2)}) collective-permute-start(f32[6,16,1,130]{3,1,2,0:T(8,128)S(1)} %get-tuple-element.44), channel_id=1, source_target_pairs={{4,0},{5,1},{6,2},{7,3},{8,4},{9,5},{10,6},{11,7},{12,8},{13,9},{1... | collective-permute-start | bytes 149768 | tf_op jit(solution)/shard_map/ppermute | solution.py:22
  78.5 3.2 %collective-permute-done.9 = f32[6,16,1,130]{3,1,2,0:T(8,128)S(1)} collective-permute-done((f32[6,16,1,130]{3,1,2,0:T(8,128)S(1)}, f32[6,16,1,130]{3,1,2,0:T(8,128)S(1)}, u32[]{:S(2)}, u32[]{:S(2)}) %collective-permute-start.9) | collective-permute-done | bytes 49952 | tf_op jit(solution)/shard_map/ppermute | solution.py:22
  84.4 4.7 %maximum_maximum_fusion.1 = (f32[6,16,33,130]{3,1,2,0:T(8,128)}, f32[6,16,33,130]{3,1,2,0:T(8,128)}) fusion(f32[6,16,32,1]{3,1,2,0:T(8,128)S(1)} %broadcast_select_fusion, f32[6,16,32,128]{3,1,2,0:T(8,128)S(1)} %copy.336, f32[6,16,32,1]{3,1,2,0:T(8,128)S(1)} %broadcast_select_fusion.1, f32[6,16,1,130]{3,1,2,0:T(8,128)S(1)} %broadcast_select_fusion.35, ...), kind=kLoop, calls=%fused_computation.3 | loop fusion | flops 2471040 | bytes 4992000 | tf_op jit(solution)/shard_map/concatenate | solution.py:78
  90.6 10.8 %collective-permute-done.11 = f32[6,1,34,130]{3,1,2,0:T(1,128)S(1)} collective-permute-done((f32[6,1,34,130]{3,1,2,0:T(1,128)S(1)}, f32[6,1,34,130]{3,1,2,0:T(1,128)S(1)}, u32[]{:S(2)}, u32[]{:S(2)}) %collective-permute-start.11) | collective-permute-done | bytes 106112 | tf_op jit(solution)/shard_map/ppermute | solution.py:22
  101.7 6.3 %maximum_maximum_fusion = (f32[6,17,34,130]{3,1,2,0:T(8,128)S(1)}, f32[6,17,34,130]{3,1,2,0:T(8,128)S(1)}) fusion(f32[6,16,1,130]{3,1,2,0:T(8,128)S(1)} %broadcast_select_fusion.34, f32[6,16,32,1]{3,1,2,0:T(8,128)S(1)} %broadcast_select_fusion, f32[6,16,32,128]{3,1,2,0:T(8,128)} %copy-done, f32[6,16,32,1]{3,1,2,0:T(8,128)} %copy-done.1, ...), kind=kLoop, calls=%fused_computation | loop fusion | flops 4508400 | bytes 5516160 | tf_op jit(solution)/shard_map/concatenate | solution.py:78
  108.2 13.5 %fusion.2 = f32[6,16,32,128]{3,1,2,0:T(8,128)} fusion(f32[6,17,34,130]{3,1,2,0:T(8,128)S(1)} %get-tuple-element.38, f32[6,16,33,130]{3,1,2,0:T(8,128)} %get-tuple-element.42, f32[6,16,32,1]{3,1,2,0:T(8,128)} %copy-done.2, f32[6,16,32,128]{3,1,2,0:T(8,128)} %copy-done, f32[6,16,32,1]{3,1,2,0:T(8,128)} %copy-done.1, f32[6,16,33,130]{3,1,2,0:T(8,128)} %get-tuple-element.41, ...), kind=kLoop, calls=%fused_computation.15 | loop fusion | flops 21233664 | bytes 42622976 | tf_op jit(solution)/shard_map/add | solution.py:59
  124.5 2.9 %broadcast_select_fusion.25 = (f32[5,16,32,128]{3,1,2,0:T(8,128)S(1)}, f32[5,16,32,128]{3,1,2,0:T(8,128)S(1)}, f32[5,16,32,128]{3,1,2,0:T(8,128)}, f32[5,16,32,1...) fusion(f32[5,16,32,128]{3,1,2,0:T(8,128)S(1)} %get-tuple-element.6, ...), kind=kLoop, calls=%fused_computation.100 | loop fusion | flops 2293760 | bytes 10944512 | tf_op jit(solution)/shard_map/jit(_where)/select_n | solution.py:66
  127.4 4.1 %broadcast_select_fusion.26 = (f32[5,16,32,128]{3,1,2,0:T(8,128)S(1)}, f32[5,16,32,128]{3,1,2,0:T(8,128)S(1)}, f32[5,16,32,128]{3,1,2,0:T(8,128)S(1)}, f32[5,16,...) fusion(f32[5,16,32,128]{3,1,2,0:T(8,128)S(1)} %get-tuple-elemen, ...), kind=kLoop, calls=%fused_computation.101 | loop fusion | flops 5898240 | bytes 26083328 | tf_op jit(solution)/shard_map/jit(_where)/select_n | solution.py:66
  131.6 18.6 %pad_add_fusion = f32[5,18,34,130]{3,1,2,0:T(8,128)S(1)} fusion(f32[5,16,32,128]{3,1,2,0:T(8,128)} %get-tuple-element.77, f32[5,16,32,128]{3,1,2,0:T(8,128)S(1)} %get-tuple-element.54, f32[5,16,32,128]{3,1,2,0:T(8,128)S(1)} %get-tuple-element.55, f32[5,16,32,128]{3,1,2,0:T(8,128)S(1)} %get-tuple-element.56, f32[5,16,32,128]{3,1,2,0:T(8,128)S(1)} %get-tuple-element.57, ...), kind=kLoop, calls=%fused_computation.2 | loop fusion | flops 10342800 | bytes 36980640 | tf_op jit(solution)/shard_map/add | solution.py:66
  151.6 2.4 %collective-permute-done.12 = f32[5,1,34,130]{3,1,2,0:T(1,128)S(1)} collective-permute-done((f32[5,1,34,130]{3,1,2,0:T(1,128)S(1)}, f32[5,1,34,130]{3,1,2,0:T(1,128)S(1)}, u32[]{:S(2)}, u32[]{:S(2)}) %collective-permute-start.12) | collective-permute-done | bytes 88432 | tf_op jit(solution)/shard_map/ppermute | solution.py:22
  156.1 5.3 %collective-permute-done.13 = f32[5,1,34,130]{3,1,2,0:T(1,128)S(1)} collective-permute-done((f32[5,1,34,130]{3,1,2,0:T(1,128)S(1)}, f32[5,1,34,130]{3,1,2,0:T(1,128)S(1)}, u32[]{:S(2)}, u32[]{:S(2)}) %collective-permute-start.13) | collective-permute-done | bytes 88432 | tf_op jit(solution)/shard_map/ppermute | solution.py:22
  163.6 4.5 %collective-permute-done.14 = f32[5,16,1,130]{3,1,2,0:T(8,128)S(1)} collective-permute-done((f32[5,16,1,130]{3,1,2,0:T(8,128)S(1)}, f32[5,16,1,130]{3,1,2,0:T(8,128)S(1)}, u32[]{:S(2)}, u32[]{:S(2)}) %collective-permute-start.14) | collective-permute-done | bytes 41632 | tf_op jit(solution)/shard_map/ppermute | solution.py:22
  179.5 9.5 %collective-permute-start.16 = (f32[5,16,32,1]{2,1,3,0:T(8,128)S(1)}, f32[5,16,32,1]{2,1,3,0:T(8,128)S(1)}, u32[]{:S(2)}, u32[]{:S(2)}) collective-permute-start(f32[5,16,32,1]{2,1,3,0:T(8,128)S(1)} %copy.339), channel_id=1, source_target_pairs={{0,1},{1,2},{2,3},{3,4},{4,5},{5,6},{6,7},{7,8},{8,9},{9,10},{10,1... | collective-permute-start | bytes 30728 | tf_op jit(solution)/shard_map/ppermute | solution.py:22
  191.7 3.3 %slice_add_fusion.1 = (f32[5,16,32,1]{3,1,2,0:T(8,128)}, f32[5,16,32,1]{3,1,2,0:T(8,128)}) fusion(f32[5,16,32,1]{3,1,2,0:T(8,128)} %copy.342, f32[5,16,32,130]{3,1,2,0:T(8,128)S(1)} %pad_maximum_fusion.4), kind=kLoop, calls=%fused_computation.70 | loop fusion | flops 2560 | bytes 51200 | tf_op jit(solution)/shard_map/add | solution.py:99
  196.8 4.6 %collective-permute-start.17 = (f32[5,16,32,1]{2,1,3,0:T(8,128)S(1)}, f32[5,16,32,1]{2,1,3,0:T(8,128)S(1)}, u32[]{:S(2)}, u32[]{:S(2)}) collective-permute-start(f32[5,16,32,1]{2,1,3,0:T(8,128)S(1)} %copy.344), channel_id=1, source_target_pairs={{1,0},{2,1},{3,2},{4,3},{5,4},{6,5},{7,6},{8,7},{9,8},{10,9},{11,1... | collective-permute-start | bytes 30728 | tf_op jit(solution)/shard_map/ppermute | solution.py:22
  208.4 2.6 %slice_add_fusion = f32[5,16,32,1]{3,1,2,0:T(8,128)} fusion(f32[5,16,32,1]{3,1,2,0:T(8,128)} %copy.347, f32[5,16,32,130]{3,1,2,0:T(8,128)S(1)} %pad_maximum_fusion.4), kind=kLoop, calls=%fused_computation.68 | loop fusion | flops 2560 | bytes 30720 | tf_op jit(solution)/shard_map/add | solution.py:101
  214.7 3.1 %maximum_divide_fusion = f32[1,5,16,32,128]{4,3,2,1,0:T(8,128)} fusion(f32[1,5,16,32,1]{4,3,2,1,0:T(8,128)} %copy.351, f32[1,5,16,32,126]{4,3,2,1,0:T(8,128)S(1)} %copy-done.4, f32[1,5,16,32,1]{4,3,2,1,0:T(8,128)S(1)} %copy-done.5, f32[16,32,128]{2,1,0:T(8,128)S(1)} %copy-done.15), kind=kLoop, calls=%fused_computation.72 | loop fusion | flops 983040 | bytes 2883584 | tf_op jit(solution)/shard_map/div | solution.py:135
  (140 shorter events, 62.4 us)
Async XLA Ops:
  2.5 105.6 %copy-start.6 = (pred[1,16,32,128]{3,1,2,0:T(8,128)(4,1)}, pred[1,16,32,128]{3,1,2,0:T(8,128)(4,1)S(1)}, u32[]{:S(2)}) copy-start(pred[1,16,32,128]{3,1,2,0:T(8,128)(4,1)S(1)} %get-tuple-element.10) | copy-start | bytes 196612
  2.5 105.6 %copy-start.7 = (pred[1,16,32,128]{3,1,2,0:T(8,128)(4,1)}, pred[1,16,32,128]{3,1,2,0:T(8,128)(4,1)S(1)}, u32[]{:S(2)}) copy-start(pred[1,16,32,128]{3,1,2,0:T(8,128)(4,1)S(1)} %get-tuple-element.8) | copy-start | bytes 196612
  8.0 5.2 %collective-permute-start = (f32[1,1,34,130]{3,1,2,0:T(1,128)S(1)}, f32[1,1,34,130]{3,1,2,0:T(1,128)S(1)}, u32[]{:S(2)}, u32[]{:S(2)}) collective-permute-start(f32[1,1,34,130]{3,1,2,0:T(1,128)S(1)} %slice.283), channel_id=1, source_target_pairs={{0,16},{1,17},{2,18},{3,19},{4,20},{5,21},{6,22},{7,23},{8,24},{9,... | collective-permute-start | bytes 53048 | tf_op jit(solution)/shard_map/ppermute | solution.py:22
  13.4 5.6 %collective-permute-start.1 = (f32[1,1,34,130]{3,1,2,0:T(1,128)S(1)}, f32[1,1,34,130]{3,1,2,0:T(1,128)S(1)}, u32[]{:S(2)}, u32[]{:S(2)}) collective-permute-start(f32[1,1,34,130]{3,1,2,0:T(1,128)S(1)} %get-tuple-element.79), channel_id=1, source_target_pairs={{16,0},{17,1},{18,2},{19,3},{20,4},{21,5},{22,6},{23,7},{24,8},{25... | collective-permute-start | bytes 53048 | tf_op jit(solution)/shard_map/ppermute | solution.py:22
  19.0 4.5 %collective-permute-start.2 = (f32[1,16,1,130]{3,1,2,0:T(8,128)S(1)}, f32[1,16,1,130]{3,1,2,0:T(8,128)S(1)}, u32[]{:S(2)}, u32[]{:S(2)}) collective-permute-start(f32[1,16,1,130]{3,1,2,0:T(8,128)S(1)} %pad_maximum_fusion.21), channel_id=1, source_target_pairs={{0,4},{1,5},{2,6},{3,7},{4,8},{5,9},{6,10},{7,11},{8,12},{9,13},{1... | collective-permute-start | bytes 24968 | tf_op jit(solution)/shard_map/ppermute | solution.py:22
  23.5 5.4 %collective-permute-start.3 = (f32[1,16,1,130]{3,1,2,0:T(8,128)S(1)}, f32[1,16,1,130]{3,1,2,0:T(8,128)S(1)}, u32[]{:S(2)}, u32[]{:S(2)}) collective-permute-start(f32[1,16,1,130]{3,1,2,0:T(8,128)S(1)} %get-tuple-element.83), channel_id=1, source_target_pairs={{4,0},{5,1},{6,2},{7,3},{8,4},{9,5},{10,6},{11,7},{12,8},{13,9},{1... | collective-permute-start | bytes 24968 | tf_op jit(solution)/shard_map/ppermute | solution.py:22
  29.2 11.3 %collective-permute-start.4 = (f32[1,16,32,1]{3,2,1,0:T(8,128)S(1)}, f32[1,16,32,1]{3,2,1,0:T(8,128)S(1)}, u32[]{:S(2)}, u32[]{:S(2)}) collective-permute-start(f32[1,16,32,1]{3,2,1,0:T(8,128)S(1)} %slice.289), channel_id=1, source_target_pairs={{0,1},{1,2},{2,3},{3,4},{4,5},{5,6},{6,7},{7,8},{8,9},{9,10},{10,1... | collective-permute-start | bytes 6152 | tf_op jit(solution)/shard_map/ppermute | solution.py:22
  40.6 8.4 %collective-permute-start.5 = (f32[1,16,32,1]{3,2,1,0:T(8,128)S(1)}, f32[1,16,32,1]{3,2,1,0:T(8,128)S(1)}, u32[]{:S(2)}, u32[]{:S(2)}) collective-permute-start(f32[1,16,32,1]{3,2,1,0:T(8,128)S(1)} %get-tuple-element.85), channel_id=1, source_target_pairs={{1,0},{2,1},{3,2},{4,3},{5,4},{6,5},{7,6},{8,7},{9,8},{10,9},{11,1... | collective-permute-start | bytes 6152 | tf_op jit(solution)/shard_map/ppermute | solution.py:22
  46.0 28.1 %copy-start.11 = (pred[1,16,32,128]{3,1,2,0:T(8,128)(4,1)}, pred[1,16,32,128]{3,1,2,0:T(8,128)(4,1)S(1)}, u32[]{:S(2)}) copy-start(pred[1,16,32,128]{3,1,2,0:T(8,128)(4,1)S(1)} %get-tuple-element.87) | copy-start | bytes 196612
  46.0 62.1 %copy-start.10 = (pred[1,16,32,128]{3,1,2,0:T(8,128)(4,1)}, pred[1,16,32,128]{3,1,2,0:T(8,128)(4,1)S(1)}, u32[]{:S(2)}) copy-start(pred[1,16,32,128]{3,1,2,0:T(8,128)(4,1)S(1)} %get-tuple-element.20) | copy-start | bytes 196612
  55.5 6.7 %collective-permute-start.6 = (f32[6,16,32,1]{2,1,3,0:T(8,128)}, f32[6,16,32,1]{2,1,3,0:T(8,128)}, u32[]{:S(2)}, u32[]{:S(2)}) collective-permute-start(f32[6,16,32,1]{2,1,3,0:T(8,128)} %copy.352), channel_id=1, source_target_pairs={{0,1},{1,2},{2,3},{3,4},{4,5},{5,6},{6,7},{7,8},{8,9},{9,10},{10,1... | collective-permute-start | bytes 36872 | tf_op jit(solution)/shard_map/ppermute | solution.py:22
  58.5 25.9 %copy-start = (f32[6,16,32,128]{3,1,2,0:T(8,128)}, f32[6,16,32,128]{3,1,2,0:T(8,128)S(1)}, u32[]{:S(2)}) copy-start(f32[6,16,32,128]{3,1,2,0:T(8,128)S(1)} %copy.336) | copy-start | bytes 4718596
  59.8 7.5 %collective-permute-start.7 = (f32[6,16,32,1]{2,1,3,0:T(8,128)}, f32[6,16,32,1]{2,1,3,0:T(8,128)}, u32[]{:S(2)}, u32[]{:S(2)}) collective-permute-start(f32[6,16,32,1]{2,1,3,0:T(8,128)} %copy.353), channel_id=1, source_target_pairs={{1,0},{2,1},{3,2},{4,3},{5,4},{6,5},{7,6},{8,7},{9,8},{10,9},{11,1... | collective-permute-start | bytes 36872 | tf_op jit(solution)/shard_map/ppermute | solution.py:22
  66.3 18.0 %copy-start.1 = (f32[6,16,32,1]{3,1,2,0:T(8,128)}, f32[6,16,32,1]{3,1,2,0:T(8,128)S(1)}, u32[]{:S(2)}) copy-start(f32[6,16,32,1]{3,1,2,0:T(8,128)S(1)} %broadcast_select_fusion.1) | copy-start | bytes 36868
  71.5 30.2 %copy-start.2 = (f32[6,16,32,1]{3,1,2,0:T(8,128)}, f32[6,16,32,1]{3,1,2,0:T(8,128)S(1)}, u32[]{:S(2)}) copy-start(f32[6,16,32,1]{3,1,2,0:T(8,128)S(1)} %broadcast_select_fusion) | copy-start | bytes 36868
  71.6 6.8 %collective-permute-start.8 = (f32[6,16,1,130]{3,1,2,0:T(8,128)S(1)}, f32[6,16,1,130]{3,1,2,0:T(8,128)S(1)}, u32[]{:S(2)}, u32[]{:S(2)}) collective-permute-start(f32[6,16,1,130]{3,1,2,0:T(8,128)S(1)} %get-tuple-element.43), channel_id=1, source_target_pairs={{0,4},{1,5},{2,6},{3,7},{4,8},{5,9},{6,10},{7,11},{8,12},{9,13},{1... | collective-permute-start | bytes 149768 | tf_op jit(solution)/shard_map/ppermute | solution.py:22
  75.5 6.2 %collective-permute-start.9 = (f32[6,16,1,130]{3,1,2,0:T(8,128)S(1)}, f32[6,16,1,130]{3,1,2,0:T(8,128)S(1)}, u32[]{:S(2)}, u32[]{:S(2)}) collective-permute-start(f32[6,16,1,130]{3,1,2,0:T(8,128)S(1)} %get-tuple-element.44), channel_id=1, source_target_pairs={{4,0},{5,1},{6,2},{7,3},{8,4},{9,5},{10,6},{11,7},{12,8},{13,9},{1... | collective-permute-start | bytes 149768 | tf_op jit(solution)/shard_map/ppermute | solution.py:22
  83.0 7.4 %collective-permute-start.10 = (f32[6,1,34,130]{3,1,2,0:T(1,128)S(1)}, f32[6,1,34,130]{3,1,2,0:T(1,128)S(1)}, u32[]{:S(2)}, u32[]{:S(2)}) collective-permute-start(f32[6,1,34,130]{3,1,2,0:T(1,128)S(1)} %get-tuple-element.39), channel_id=1, source_target_pairs={{0,16},{1,17},{2,18},{3,19},{4,20},{5,21},{6,22},{7,23},{8,24},{9,... | collective-permute-start | bytes 318248 | tf_op jit(solution)/shard_map/ppermute | solution.py:22
  89.1 12.3 %collective-permute-start.11 = (f32[6,1,34,130]{3,1,2,0:T(1,128)S(1)}, f32[6,1,34,130]{3,1,2,0:T(1,128)S(1)}, u32[]{:S(2)}, u32[]{:S(2)}) collective-permute-start(f32[6,1,34,130]{3,1,2,0:T(1,128)S(1)} %get-tuple-element.40), channel_id=1, source_target_pairs={{16,0},{17,1},{18,2},{19,3},{20,4},{21,5},{22,6},{23,7},{24,8},{25... | collective-permute-start | bytes 318248 | tf_op jit(solution)/shard_map/ppermute | solution.py:22
  101.6 6.5 %copy-start.12 = (pred[1,16,32,128]{3,1,2,0:T(8,128)(4,1)S(1)}, pred[1,16,32,128]{3,1,2,0:T(8,128)(4,1)}, u32[]{:S(2)}) copy-start(pred[1,16,32,128]{3,1,2,0:T(8,128)(4,1)} %copy-done.11) | copy-start | bytes 196612
  101.6 6.5 %copy-start.14 = (pred[1,16,32,128]{3,1,2,0:T(8,128)(4,1)S(1)}, pred[1,16,32,128]{3,1,2,0:T(8,128)(4,1)}, u32[]{:S(2)}) copy-start(pred[1,16,32,128]{3,1,2,0:T(8,128)(4,1)} %get-tuple-element.95) | copy-start | bytes 196612
  101.7 6.5 %copy-start.16 = (pred[16,32,128]{2,0,1:T(8,128)(4,1)S(1)}, pred[16,32,128]{2,0,1:T(8,128)(4,1)}, u32[]{:S(2)}) copy-start(pred[16,32,128]{2,0,1:T(8,128)(4,1)} %get-tuple-element.7) | copy-start | bytes 196612
  101.7 6.5 %copy-start.17 = (pred[16,32,128]{2,0,1:T(8,128)(4,1)S(1)}, pred[16,32,128]{2,0,1:T(8,128)(4,1)}, u32[]{:S(2)}) copy-start(pred[16,32,128]{2,0,1:T(8,128)(4,1)} %get-tuple-element.97) | copy-start | bytes 196612
  101.7 6.5 %copy-start.18 = (pred[16,32,128]{2,0,1:T(8,128)(4,1)S(1)}, pred[16,32,128]{2,0,1:T(8,128)(4,1)}, u32[]{:S(2)}) copy-start(pred[16,32,128]{2,0,1:T(8,128)(4,1)} %get-tuple-element.98) | copy-start | bytes 196612
  101.7 6.5 %copy-start.19 = (pred[16,32,128]{2,0,1:T(8,128)(4,1)S(1)}, pred[16,32,128]{2,0,1:T(8,128)(4,1)}, u32[]{:S(2)}) copy-start(pred[16,32,128]{2,0,1:T(8,128)(4,1)} %get-tuple-element.100) | copy-start | bytes 196612
  101.7 6.5 %copy-start.20 = (pred[16,32,128]{2,0,1:T(8,128)(4,1)S(1)}, pred[16,32,128]{2,0,1:T(8,128)(4,1)}, u32[]{:S(2)}) copy-start(pred[16,32,128]{2,0,1:T(8,128)(4,1)} %get-tuple-element.101) | copy-start | bytes 196612
  150.3 3.7 %collective-permute-start.12 = (f32[5,1,34,130]{3,1,2,0:T(1,128)S(1)}, f32[5,1,34,130]{3,1,2,0:T(1,128)S(1)}, u32[]{:S(2)}, u32[]{:S(2)}) collective-permute-start(f32[5,1,34,130]{3,1,2,0:T(1,128)S(1)} %slice.324), channel_id=1, source_target_pairs={{0,16},{1,17},{2,18},{3,19},{4,20},{5,21},{6,22},{7,23},{8,24},{9,... | collective-permute-start | bytes 265208 | tf_op jit(solution)/shard_map/ppermute | solution.py:22
  154.3 7.1 %collective-permute-start.13 = (f32[5,1,34,130]{3,1,2,0:T(1,128)S(1)}, f32[5,1,34,130]{3,1,2,0:T(1,128)S(1)}, u32[]{:S(2)}, u32[]{:S(2)}) collective-permute-start(f32[5,1,34,130]{3,1,2,0:T(1,128)S(1)} %get-tuple-element.46), channel_id=1, source_target_pairs={{16,0},{17,1},{18,2},{19,3},{20,4},{21,5},{22,6},{23,7},{24,8},{25... | collective-permute-start | bytes 265208 | tf_op jit(solution)/shard_map/ppermute | solution.py:22
  161.6 6.4 %collective-permute-start.14 = (f32[5,16,1,130]{3,1,2,0:T(8,128)S(1)}, f32[5,16,1,130]{3,1,2,0:T(8,128)S(1)}, u32[]{:S(2)}, u32[]{:S(2)}) collective-permute-start(f32[5,16,1,130]{3,1,2,0:T(8,128)S(1)} %pad_maximum_fusion.19), channel_id=1, source_target_pairs={{0,4},{1,5},{2,6},{3,7},{4,8},{5,9},{6,10},{7,11},{8,12},{9,13},{1... | collective-permute-start | bytes 124808 | tf_op jit(solution)/shard_map/ppermute | solution.py:22
  168.1 6.1 %collective-permute-start.15 = (f32[5,16,1,130]{3,1,2,0:T(8,128)S(1)}, f32[5,16,1,130]{3,1,2,0:T(8,128)S(1)}, u32[]{:S(2)}, u32[]{:S(2)}) collective-permute-start(f32[5,16,1,130]{3,1,2,0:T(8,128)S(1)} %get-tuple-element.48), channel_id=1, source_target_pairs={{4,0},{5,1},{6,2},{7,3},{8,4},{9,5},{10,6},{11,7},{12,8},{13,9},{1... | collective-permute-start | bytes 124808 | tf_op jit(solution)/shard_map/ppermute | solution.py:22
  179.5 10.6 %collective-permute-start.16 = (f32[5,16,32,1]{2,1,3,0:T(8,128)S(1)}, f32[5,16,32,1]{2,1,3,0:T(8,128)S(1)}, u32[]{:S(2)}, u32[]{:S(2)}) collective-permute-start(f32[5,16,32,1]{2,1,3,0:T(8,128)S(1)} %copy.339), channel_id=1, source_target_pairs={{0,1},{1,2},{2,3},{3,4},{4,5},{5,6},{6,7},{7,8},{8,9},{9,10},{10,1... | collective-permute-start | bytes 30728 | tf_op jit(solution)/shard_map/ppermute | solution.py:22
  196.8 10.0 %collective-permute-start.17 = (f32[5,16,32,1]{2,1,3,0:T(8,128)S(1)}, f32[5,16,32,1]{2,1,3,0:T(8,128)S(1)}, u32[]{:S(2)}, u32[]{:S(2)}) collective-permute-start(f32[5,16,32,1]{2,1,3,0:T(8,128)S(1)} %copy.344), channel_id=1, source_target_pairs={{1,0},{2,1},{3,2},{4,3},{5,4},{6,5},{7,6},{8,7},{9,8},{10,9},{11,1... | collective-permute-start | bytes 30728 | tf_op jit(solution)/shard_map/ppermute | solution.py:22
  (16 other events, 49.4 us)
where the time goes:
time: 219 us; the launch traced here: 218 us
  other arithmetic  82.3 us (38%)
  starting transfers between devices  55.9 us (26%)
  waiting for transfers between devices  45.4 us (21%)
  local copies, waits for them, and re-layouts  33.2 us (15%)
    ppermute x18, starting transfers between devices, shifted(): return lax.ppermute(shard, axis, pairs)  55.9 us
    ppermute x18, waiting for transfers between devices, shifted(): return lax.ppermute(shard, axis, pairs)  45.4 us
    add x1, other arithmetic, spread_back(): running = running + placed(jnp.where(inside[None], average, 0.0), offset)  18.6 us
    add x1, other arithmetic, neighbour_average(): running + jnp.where(inside[None], window(weighted, offset, interior), 0.0)  13.5 us
    concatenate x2, other arithmetic, exchange_rims(): return jnp.concatenate([from_below, values, from_above], axis=spatial_dim)  11.1 us
    select_n x3, other arithmetic, spread_back(): running = running + placed(jnp.where(inside[None], average, 0.0), offset)  8.69 us
    unnamed x60, local copies, waits for them, and re-layouts  5.53 us
    ppermute x2, local copies, waits for them, and re-layouts, shifted(): return lax.ppermute(shard, axis, pairs)  5.25 us
  transfers between devices with their start and end apart: 18, of which 14 were waited for; matrix products, arithmetic and copies ran while one was open for 10% of the time, Pallas kernels for 0%

commit v1 on v0

v1 whole, which is shorter than its diff:
```python
import functools

import jax
import jax.numpy as jnp
from jax import lax
from jax.experimental import pallas as pl
from jax.experimental.pallas import tpu as pltpu
from jax.sharding import PartitionSpec as P

NBY = 4
NBZ = 4
MESH = pl.DeviceIdType.MESH
XP, XM, YP, YM, ZP, ZM = 1, 2, 4, 8, 16, 32
ONE, UP, DOWN = 10, 14, 18
PX, PY = 3, 8


def flag(ax, ay, az):
    return (
        {1: XP, -1: XM, 0: 0}[ax] | {1: YP, -1: YM, 0: 0}[ay] | {1: ZP, -1: ZM, 0: 0}[az]
    )


def holds(e, bits):
    return (e & bits) == bits


def kernel(n, dims, u_ref, vf_ref, mask_ref, code_ref, out_ref, ext_e, ext_f, cnt, w0, wp, wm, avg,
           raw_m, raw_c, ys_e, ys_f, yr_e, yr_f, cr_e, cr_f, zs, zr, load_sem, send_sem, recv_sem):
    fields, cx, cy, cz = dims
    chans = fields + 1
    me = lax.axis_index("boxes")
    bx, by, bz = me // (NBY * NBZ), me // NBZ % NBY, me % NBZ
    axes = {
        "x": (NBY * NBZ, bx > 0, bx < n // (NBY * NBZ) - 1),
        "y": (NBZ, by > 0, by < NBY - 1),
        "z": (1, bz > 0, bz < NBZ - 1),
    }
    lane = lax.broadcasted_iota(jnp.int32, (8, cz), 1)
    nyb = (cy + 8) // 8

    loads = [
        pltpu.make_async_copy(mask_ref.at[0], raw_m, load_sem.at[0]),
        pltpu.make_async_copy(code_ref.at[0], raw_c, load_sem.at[1]),
        pltpu.make_async_copy(vf_ref.at[0], ext_f.at[0, PX:PX + cx, PY:PY + cy], load_sem.at[2]),
        pltpu.make_async_copy(u_ref.at[0], ext_f.at[1:chans, PX:PX + cx, PY:PY + cy], load_sem.at[3]),
    ]
    for copy in loads:
        copy.start()

    barrier = pltpu.get_barrier_semaphore()
    total = jnp.int32(0)
    for stride, low, high in axes.values():
        for has, there in ((low, me - stride), (high, me + stride)):
            @pl.when(has)
            def _():
                pl.semaphore_signal(barrier, inc=1, device_id=(there,), device_id_type=MESH)
            total = total + has.astype(jnp.int32)
    pl.semaphore_wait(barrier, total)

    def copies(axis, ident, up, down):
        stride = axes[axis][0]
        out = []
        for d, (pair, there) in enumerate(((up, me + stride), (down, me - stride))):
            out.append(pltpu.make_async_remote_copy(
                src_ref=pair[0], dst_ref=pair[1], send_sem=send_sem.at[2 * ident + d],
                recv_sem=recv_sem.at[2 * ident + d], device_id=(there,), device_id_type=MESH))
        return axis, out

    def start(c):
        axis, (up, down) = c
        _, low, high = axes[axis]
        pl.when(high)(lambda: up.start())
        pl.when(low)(lambda: down.start())

    def recv(c):
        axis, (up, down) = c
        _, low, high = axes[axis]
        pl.when(low)(lambda: up.wait_recv())
        pl.when(high)(lambda: down.wait_recv())

    def sent(c):
        axis, (up, down) = c
        _, low, high = axes[axis]
        pl.when(high)(lambda: up.wait_send())
        pl.when(low)(lambda: down.wait_send())

    def x_face(ident, ref, lead, depth):
        box = slice(PY, PY + cy)
        at = lambda a, b: ref.at[lead + (slice(a, b), box)]
        end = PX + cx
        return copies("x", ident, (at(end - depth, end), at(PX - depth, PX)),
                      (at(PX, PX + depth), at(end, end + depth)))

    x_e = x_face(0, ext_e, (), 3)
    x_vf = x_face(1, ext_f, (slice(0, 1),), 2)
    x_u = x_face(2, ext_f, (slice(1, chans),), 2)
    y_e = copies("y", 3, (ys_e.at[0], yr_e.at[0]), (ys_e.at[1], yr_e.at[1]))
    y_f = copies("y", 4, (ys_f.at[0], yr_f.at[0]), (ys_f.at[1], yr_f.at[1]))
    c_e = copies("x", 5, (yr_e.at[:, cx - 3:cx], cr_e.at[0]), (yr_e.at[:, 0:3], cr_e.at[1]))
    c_f = copies("x", 6, (yr_f.at[:, :, cx - 2:cx], cr_f.at[0]), (yr_f.at[:, :, 0:2], cr_f.at[1]))
    spans = ((0, 1), (1, 1 + chans), (1 + chans, 1 + chans + fields))
    z_c = [copies("z", 7 + i, (zs.at[0, a:b], zr.at[0, a:b]), (zs.at[1, a:b], zr.at[1, a:b]))
           for i, (a, b) in enumerate(spans)]
    everything = [x_e, x_vf, x_u, y_e, y_f, c_e, c_f] + z_c

    loads[0].wait()
    loads[1].wait()

    def encode(p, _):
        c = raw_c[p]
        cut = raw_m[p] == 1
        third = (c * 171) >> 9
        sz = c - 3 * third
        ninth = (third * 171) >> 9
        sy = third - 3 * ninth
        bit = lambda test, value: jnp.where(test, value, 0)
        e = (bit(ninth == 2, XP) + bit(ninth == 0, XM) + bit(sy == 2, YP) + bit(sy == 0, YM)
             + bit(sz == 2, ZP + (1 << UP)) + bit(sz == 0, ZM + (1 << DOWN)))
        ext_e[PX + p, PY:PY + cy, :] = jnp.where(cut, e, 0) + (1 << ONE)
        return 0

    lax.fori_loop(0, cx, encode, 0)
    start(x_e)
    ys_e[0] = ext_e[PX:PX + cx, PY + cy - 4:PY + cy, :]
    ys_e[1] = ext_e[PX:PX + cx, PY:PY + 4, :]
    start(y_e)
    loads[2].wait()
    start(x_vf)
    loads[3].wait()
    start(x_u)
    for c in range(chans):
        ys_f[0, c] = ext_f[c, PX:PX + cx, PY + cy - 2:PY + cy, :]
        ys_f[1, c] = ext_f[c, PX:PX + cx, PY:PY + 2, :]
    start(y_f)

    end = PX + cx
    _, low, high = axes["x"]
    for has, (e0, e1), (f0, f1) in ((low, (0, 3), (1, 3)), (high, (end, end + 3), (end, end + 2))):
        @pl.when(jnp.logical_not(has))
        def _():
            ext_e[e0:e1, :, :] = jnp.full((e1 - e0,) + ext_e.shape[1:], 1 << ONE, jnp.int32)
            for c in range(chans):
                ext_f[c, f0:f1, :, :] = jnp.zeros((f1 - f0,) + ext_f.shape[2:], jnp.float32)
    _, low, high = axes["y"]
    for side, has in enumerate((low, high)):
        @pl.when(jnp.logical_not(has))
        def _():
            yr_e[side] = jnp.full(yr_e.shape[1:], 1 << ONE, jnp.int32)
            yr_f[side] = jnp.zeros(yr_f.shape[1:], jnp.float32)
    _, low, high = axes["z"]
    for side, has in enumerate((low, high)):
        @pl.when(jnp.logical_not(has))
        def _():
            zr[side] = jnp.zeros(zr.shape[1:], jnp.float32)

    recv(y_e)
    start(c_e)
    ext_e[PX:PX + cx, PY - 4:PY, :] = yr_e[0]
    ext_e[PX:PX + cx, PY + cy:PY + cy + 4, :] = yr_e[1]
    recv(y_f)
    start(c_f)
    for c in range(chans):
        ext_f[c, PX:PX + cx, PY - 2:PY, :] = yr_f[0, c]
        ext_f[c, PX:PX + cx, PY + cy:PY + cy + 2, :] = yr_f[1, c]
    for c in (x_e, c_e, x_vf, x_u, c_f):
        recv(c)
    _, low, high = axes["x"]
    for side, has, e0, f0 in ((0, low, 0, 1), (1, high, end, end)):
        @pl.when(has)
        def _():
            for ys, er, fr in ((0, PY - 4, PY - 2), (1, PY + cy, PY + cy)):
                ext_e[e0:e0 + 3, er:er + 4, :] = cr_e[side, ys]
                for c in range(chans):
                    ext_f[c, f0:f0 + 2, fr:fr + 2, :] = cr_f[side, ys, c]

    def blocks(p0, p1, count, row0, body):
        def plane(p, _):
            def block(b, _):
                body(p, row0 + 8 * b, (p - p0) * count + b)
                return 0
            return lax.fori_loop(0, count, block, 0)
        lax.fori_loop(p0, p1, plane, 0)

    def rows(ref, lead, p, r):
        return ref[lead + (p, pl.ds(r, 8), slice(None))]

    def pack(slot, k, to_upper, to_lower):
        here = lane == k
        zs[0, slot] = jnp.where(here, pltpu.roll(to_upper, lax.rem(k + 1, cz), 1), zs[0, slot])
        zs[1, slot] = jnp.where(here, pltpu.roll(to_lower, k, 1), zs[1, slot])

    def from_lower(slot, k):
        return pltpu.roll(zr[0, slot], lax.rem(cz - k, cz), 1)

    def from_upper(slot, k):
        return pltpu.roll(zr[1, slot], cz - 1 - k, 1)

    pairs = [(ax, ay) for ax in (-1, 0, 1) for ay in (-1, 0, 1)]

    def count_body(p, r, k):
        acc = rows(ext_e, (), p, r)
        for ax, ay in pairs:
            if (ax, ay) != (0, 0):
                e = rows(ext_e, (), p - ax, r - ay)
                acc = acc + jnp.where(holds(e, flag(ax, ay, 0)), e, 0)
        up, down = (acc >> UP) & 15, (acc >> DOWN) & 15
        inner = ((acc >> ONE) & 15) + jnp.where(lane == 0, 0, pltpu.roll(up, 1, 1))
        inner = inner + jnp.where(lane == cz - 1, 0, pltpu.roll(down, cz - 1, 1))
        cnt[p, pl.ds(r, 8), :] = inner.astype(jnp.float32)
        pack(0, k, up.astype(jnp.float32), down.astype(jnp.float32))

    blocks(PX - 2, end + 2, nyb, PY - 4, count_body)
    start(z_c[0])
    recv(z_c[0])

    def weight_body(p, r, k):
        c = rows(cnt, (), p, r)
        c = c + jnp.where(lane == 0, from_lower(0, k), 0.0)
        c = c + jnp.where(lane == cz - 1, from_upper(0, k), 0.0)
        cnt[p, pl.ds(r, 8), :] = c
        w = rows(ext_f, (0,), p, r) / c
        for ch in range(chans):
            v = w if ch == 0 else w * rows(ext_f, (ch,), p, r)
            w0[ch, p, pl.ds(r, 8), :] = v
            pack(1 + ch, k, v, v)

    blocks(PX - 2, end + 2, nyb, PY - 4, weight_body)
    start(z_c[1])
    recv(z_c[1])

    def shift_body(p, r, k):
        for ch in range(chans):
            v = rows(w0, (ch,), p, r)
            wp[ch, p, pl.ds(r, 8), :] = jnp.where(
                lane == cz - 1, from_upper(1 + ch, k), pltpu.roll(v, cz - 1, 1))
            wm[ch, p, pl.ds(r, 8), :] = jnp.where(
                lane == 0, from_lower(1 + ch, k), pltpu.roll(v, 1, 1))

    blocks(PX - 2, end + 2, nyb, PY - 4, shift_body)

    def average_body(p, r, k):
        e = rows(ext_e, (), p, r)
        m = {b: holds(e, b) for b in (XP, XM, YP, YM, ZP, ZM)}

        def along_z(ch, q, s):
            side = jnp.where(m[ZP], rows(wp, (ch,), q, s), jnp.where(m[ZM], rows(wm, (ch,), q, s), 0.0))
            return rows(w0, (ch,), q, s) + side

        def along_y(ch, q):
            side = jnp.where(m[YP], along_z(ch, q, r + 1), jnp.where(m[YM], along_z(ch, q, r - 1), 0.0))
            return along_z(ch, q, r) + side

        def whole(ch):
            side = jnp.where(m[XP], along_y(ch, p + 1), jnp.where(m[XM], along_y(ch, p - 1), 0.0))
            return along_y(ch, p) + side

        inverse = 1.0 / whole(0)
        for ch in range(1, chans):
            avg[ch - 1, p, pl.ds(r, 8), :] = whole(ch) * inverse

    blocks(PX - 1, end + 1, nyb, PY - 4, average_body)

    def deposit_body(p, r, k):
        acc = [[None] * 3 for _ in range(fields)]
        for ax, ay in pairs:
            e = rows(ext_e, (), p - ax, r - ay)
            ms = [holds(e, flag(ax, ay, az)) for az in (0, 1, -1)]
            for f in range(fields):
                v = rows(avg, (f,), p - ax, r - ay)
                for i in range(3):
                    term = v if (ax, ay, i) == (0, 0, 0) else jnp.where(ms[i], v, 0.0)
                    acc[f][i] = term if acc[f][i] is None else acc[f][i] + term
        for f in range(fields):
            here, up, down = acc[f]
            here = here + jnp.where(lane == 0, 0.0, pltpu.roll(up, 1, 1))
            here = here + jnp.where(lane == cz - 1, 0.0, pltpu.roll(down, cz - 1, 1))
            out_ref[0, f, p - PX, pl.ds(r - PY, 8), :] = here
            pack(1 + chans + f, k, up, down)

    blocks(PX, end, cy // 8, PY, deposit_body)
    start(z_c[2])
    recv(z_c[2])

    def final_body(p, r, k):
        inverse = 1.0 / rows(cnt, (), p, r)
        for f in range(fields):
            v = out_ref[0, f, p - PX, pl.ds(r - PY, 8), :]
            v = v + jnp.where(lane == 0, from_lower(1 + chans + f, k), 0.0)
            v = v + jnp.where(lane == cz - 1, from_upper(1 + chans + f, k), 0.0)
            out_ref[0, f, p - PX, pl.ds(r - PY, 8), :] = v * inverse

    blocks(PX, end, cy // 8, PY, final_body)
    for c in everything:
        sent(c)


def per_device(n, conserved, volume_fraction, cut_mask, merge_code):
    fields, cx, cy, cz = conserved.shape[1:]
    chans = fields + 1
    ext = (cx + 6, cy + 16, cz)
    f32, i32 = jnp.float32, jnp.int32
    scratch = [
        pltpu.VMEM(ext, i32), pltpu.VMEM((chans,) + ext, f32), pltpu.VMEM(ext, f32),
        pltpu.VMEM((chans,) + ext, f32), pltpu.VMEM((chans,) + ext, f32), pltpu.VMEM((chans,) + ext, f32),
        pltpu.VMEM((fields,) + ext, f32),
        pltpu.VMEM((cx, cy, cz), i32), pltpu.VMEM((cx, cy, cz), i32),
        pltpu.VMEM((2, cx, 4, cz), i32), pltpu.VMEM((2, chans, cx, 2, cz), f32),
        pltpu.VMEM((2, cx, 4, cz), i32), pltpu.VMEM((2, chans, cx, 2, cz), f32),
        pltpu.VMEM((2, 2, 3, 4, cz), i32), pltpu.VMEM((2, 2, chans, 2, 2, cz), f32),
        pltpu.VMEM((2, 1 + chans + fields, 8, cz), f32), pltpu.VMEM((2, 1 + chans + fields, 8, cz), f32),
        pltpu.SemaphoreType.DMA((4,)), pltpu.SemaphoreType.DMA((20,)), pltpu.SemaphoreType.DMA((20,)),
    ]
    return pl.pallas_call(
        functools.partial(kernel, n, (fields, cx, cy, cz)),
        out_shape=jax.ShapeDtypeStruct(conserved.shape, f32),
        in_specs=[pl.BlockSpec(memory_space=pl.ANY)] * 4,
        out_specs=pl.BlockSpec(memory_space=pltpu.VMEM),
        scratch_shapes=scratch,
        compiler_params=pltpu.CompilerParams(
            collective_id=0, has_side_effects=True, vmem_limit_bytes=48 * 1024 * 1024),
        name="redistribute",
    )(conserved, volume_fraction, cut_mask, merge_code)


def solution(mesh):
    return jax.shard_map(
        functools.partial(per_device, mesh.shape["boxes"]),
        mesh=mesh,
        in_specs=(
            P("boxes", None, None, None, None),
            P("boxes", None, None, None),
            P("boxes", None, None, None),
            P("boxes", None, None, None),
        ),
        out_specs=P("boxes", None, None, None, None),
        check_vma=False,
    )
```

time: 219 us -> 87.4 us (0.40)
  other arithmetic: 82.3 us -> 0 us
  Pallas kernels: 0 us -> 81.1 us
  starting transfers between devices: 55.9 us -> 0 us
  waiting for transfers between devices: 45.4 us -> 0 us
  local copies, waits for them, and re-layouts: 33.2 us -> 5.22 us
    pallas_call x0 -> x1, Pallas kernels: none -> 81.1 us  [per_device(): pl.pallas_call(functools.partial(kernel, n, (fields, cx, cy, cz)), out_sh...]
    ppermute x18 -> x0, starting transfers between devices: 55.9 us -> none  [shifted(): return lax.ppermute(shard, axis, pairs)]
    ppermute x18 -> x0, waiting for transfers between devices: 45.4 us -> none  [shifted(): return lax.ppermute(shard, axis, pairs)]
    add x14 -> x0, other arithmetic: 38.9 us -> none  [the longest x1 18.6 us: spread_back(): running = running + placed(jnp.where(inside[None], average, 0.0), offset)]
    concatenate x8 -> x0, other arithmetic: 14.2 us -> none  [the longest x2 11.1 us: exchange_rims(): return jnp.concatenate([from_below, values, from_above], axis=spatial_dim)]
    select_n x11 -> x0, other arithmetic: 12.2 us -> none  [the longest x3 8.69 us: spread_back(): running = running + placed(jnp.where(inside[None], average, 0.0), offset)]
    broadcast_in_dim x4 -> x0, other arithmetic: 8.91 us -> none  [the longest x3 5.08 us: neighbour_average(): jnp.where(inside[None], window(weighted, offset, interior), 0.0)]
    slice x13 -> x0, local copies, waits for them, and re-layouts: 8.2 us -> none  [the longest x5 3.65 us: return_rims(): upper_ghost = lax.slice_in_dim(values, extent - 1, extent, axis=spatial_dim)]
  transfers between devices with their start and end apart: 18 -> 0, of which waited for: 14 -> 0; matrix products, arithmetic and copies ran while one was open for 10% -> 0% of each run, Pallas kernels for 0% -> 0%
where the time goes in v1:
time: 87.4 us; the launch traced here: 86.3 us
  Pallas kernels  81.1 us (93%)
  local copies, waits for them, and re-layouts  5.22 us (6%)
    pallas_call x1, Pallas kernels, per_device(): pl.pallas_call(functools.partial(kernel, n, (fields, cx, cy, cz)), out_sh...  81.1 us
    unnamed x9, local copies, waits for them, and re-layouts  5.22 us

profile of v1, /device:TPU:5, one launch (start us, length us, event | category | flops | bytes accessed | tf_op | source)
XLA Modules:
  0.0 86.3 jit_solution(16335750934727143608)
XLA Ops:
  0.0 0.0 copy-start
  0.0 1.3 %copy-done = f32[1,5,16,32,128]{4,3,2,1,0:T(8,128)S(1)} copy-done((f32[1,5,16,32,128]{4,3,2,1,0:T(8,128)S(1)}, f32[1,5,16,32,128]{4,3,2,1,0:T(8,128)}, u32[]{:S(2)}) %copy-start) | copy-done | bytes 1310744
  1.3 0.0 copy-start.1
  1.3 0.9 %copy-done.1 = f32[1,16,32,128]{3,2,1,0:T(8,128)S(1)} copy-done((f32[1,16,32,128]{3,2,1,0:T(8,128)S(1)}, f32[1,16,32,128]{3,2,1,0:T(8,128)}, u32[]{:S(2)}) %copy-start.1) | copy-done | bytes 262168
  2.3 0.0 copy-start.2
  2.3 0.9 %copy-done.2 = s32[1,16,32,128]{3,2,1,0:T(8,128)S(1)} copy-done((s32[1,16,32,128]{3,2,1,0:T(8,128)S(1)}, s32[1,16,32,128]{3,2,1,0:T(8,128)}, u32[]{:S(2)}) %copy-start.2) | copy-done | bytes 262168
  3.2 0.0 copy-start.3
  3.2 0.9 %copy-done.3 = s32[1,16,32,128]{3,2,1,0:T(8,128)S(1)} copy-done((s32[1,16,32,128]{3,2,1,0:T(8,128)S(1)}, s32[1,16,32,128]{3,2,1,0:T(8,128)}, u32[]{:S(2)}) %copy-start.3) | copy-done | bytes 262168
  4.2 81.1 %redistribute.1 = f32[1,5,16,32,128]{4,3,2,1,0:T(8,128)S(1)} custom-call(f32[1,5,16,32,128]{4,3,2,1,0:T(8,128)S(1)} %copy-done, f32[1,16,32,128]{3,2,1,0:T(8,128)S(1)} %copy-done.1, s32[1,16,32,128]{3,2,1,0:T(8,128)S(1)} %copy-done.2, s32[1,16,32,128]{3,2,1,0:T(8,128)S(1)} %copy-done.3), custom_call_target="tpu_custom_call" | custom-call | tf_op jit(solution)/shard_map/redistribute/pallas_call | solution.py:314
  85.3 1.1 %copy.6 = f32[1,5,16,32,128]{4,3,2,1,0:T(8,128)} copy(f32[1,5,16,32,128]{4,3,2,1,0:T(8,128)S(1)} %redistribute.1) | data formatting | bytes 2621440
Async XLA Ops:
  0.0 1.3 %copy-start = (f32[1,5,16,32,128]{4,3,2,1,0:T(8,128)S(1)}, f32[1,5,16,32,128]{4,3,2,1,0:T(8,128)}, u32[]{:S(2)}) copy-start(f32[1,5,16,32,128]{4,3,2,1,0:T(8,128)} %u_ref.1) | copy-start | bytes 3932164
  1.3 0.9 %copy-start.1 = (f32[1,16,32,128]{3,2,1,0:T(8,128)S(1)}, f32[1,16,32,128]{3,2,1,0:T(8,128)}, u32[]{:S(2)}) copy-start(f32[1,16,32,128]{3,2,1,0:T(8,128)} %vf_ref.1) | copy-start | bytes 786436
  2.3 0.9 %copy-start.2 = (s32[1,16,32,128]{3,2,1,0:T(8,128)S(1)}, s32[1,16,32,128]{3,2,1,0:T(8,128)}, u32[]{:S(2)}) copy-start(s32[1,16,32,128]{3,2,1,0:T(8,128)} %mask_ref.1) | copy-start | bytes 786436
  3.2 0.9 %copy-start.3 = (s32[1,16,32,128]{3,2,1,0:T(8,128)S(1)}, s32[1,16,32,128]{3,2,1,0:T(8,128)}, u32[]{:S(2)}) copy-start(s32[1,16,32,128]{3,2,1,0:T(8,128)} %code_ref.1) | copy-start | bytes 786436

commit v2 on v1

--- a/solution.py
+++ b/solution.py
@@ -99,7 +99,8 @@
     y_f = copies("y", 4, (ys_f.at[0], yr_f.at[0]), (ys_f.at[1], yr_f.at[1]))
     c_e = copies("x", 5, (yr_e.at[:, cx - 3:cx], cr_e.at[0]), (yr_e.at[:, 0:3], cr_e.at[1]))
     c_f = copies("x", 6, (yr_f.at[:, :, cx - 2:cx], cr_f.at[0]), (yr_f.at[:, :, 0:2], cr_f.at[1]))
-    spans = ((0, 1), (1, 1 + chans), (1 + chans, 1 + chans + fields))
+    last = 1 + 2 * chans
+    spans = ((0, 1), (1, 1 + chans), (1 + chans, last), (last, last + fields))
     z_c = [copies("z", 7 + i, (zs.at[0, a:b], zr.at[0, a:b]), (zs.at[1, a:b], zr.at[1, a:b]))
            for i, (a, b) in enumerate(spans)]
     everything = [x_e, x_vf, x_u, y_e, y_f, c_e, c_f] + z_c
@@ -163,32 +164,53 @@
     for c in range(chans):
         ext_f[c, PX:PX + cx, PY - 2:PY, :] = yr_f[0, c]
         ext_f[c, PX:PX + cx, PY + cy:PY + cy + 2, :] = yr_f[1, c]
-    for c in (x_e, c_e, x_vf, x_u, c_f):
-        recv(c)
-    _, low, high = axes["x"]
-    for side, has, e0, f0 in ((0, low, 0, 1), (1, high, end, end)):
+    recv(x_e)
+    recv(c_e)
+    x_sides = [(side, has, at) for side, (has, at) in enumerate(zip(axes["x"][1:], (PX, end)))]
+    for side, has, at in x_sides:
         @pl.when(has)
         def _():
-            for ys, er, fr in ((0, PY - 4, PY - 2), (1, PY + cy, PY + cy)):
+            e0 = at - 3 if side == 0 else at
+            for ys, er in ((0, PY - 4), (1, PY + cy)):
                 ext_e[e0:e0 + 3, er:er + 4, :] = cr_e[side, ys]
-                for c in range(chans):
-                    ext_f[c, f0:f0 + 2, fr:fr + 2, :] = cr_f[side, ys, c]
-
-    def blocks(p0, p1, count, row0, body):
-        def plane(p, _):
-            def block(b, _):
-                body(p, row0 + 8 * b, (p - p0) * count + b)
-                return 0
-            return lax.fori_loop(0, count, block, 0)
-        lax.fori_loop(p0, p1, plane, 0)
+
+    zero = me // n
+
+    def blocks(planes, p0, count, row0, body):
+        steps, plane_of = planes
+        group = count
+
+        def several(p, b0, size):
+            packs = []
+            for i in range(size):
+                b = b0 + i
+                k = (p - p0) * count + b
+                packs.append((k, body(p, row0 + zero + 8 * b, k)))
+            for j in range(len(packs[0][1])):
+                slot = packs[0][1][j][0]
+                upper, lower = zs[0, slot], zs[1, slot]
+                for k, found in packs:
+                    _, to_upper, to_lower = found[j]
+                    here = lane == k
+                    upper = jnp.where(here, pltpu.roll(to_upper, lax.rem(k + 1, cz), 1), upper)
+                    lower = jnp.where(here, pltpu.roll(to_lower, k, 1), lower)
+                zs[0, slot] = upper
+                zs[1, slot] = lower
+
+        def plane(i, _):
+            several(plane_of(i), 0, count)
+            return 0
+
+        lax.fori_loop(0, steps, plane, 0)
+
+    def span(p0, p1):
+        return p1 - p0, lambda i: i + p0
+
+    def both_ends(p0, p1):
+        return 4, lambda i: i + p0 + i // 2 * (p1 - p0 - 4)
 
     def rows(ref, lead, p, r):
         return ref[lead + (p, pl.ds(r, 8), slice(None))]
-
-    def pack(slot, k, to_upper, to_lower):
-        here = lane == k
-        zs[0, slot] = jnp.where(here, pltpu.roll(to_upper, lax.rem(k + 1, cz), 1), zs[0, slot])
-        zs[1, slot] = jnp.where(here, pltpu.roll(to_lower, k, 1), zs[1, slot])
 
     def from_lower(slot, k):
         return pltpu.roll(zr[0, slot], lax.rem(cz - k, cz), 1)
@@ -208,36 +230,33 @@
         inner = ((acc >> ONE) & 15) + jnp.where(lane == 0, 0, pltpu.roll(up, 1, 1))
         inner = inner + jnp.where(lane == cz - 1, 0, pltpu.roll(down, cz - 1, 1))
         cnt[p, pl.ds(r, 8), :] = inner.astype(jnp.float32)
-        pack(0, k, up.astype(jnp.float32), down.astype(jnp.float32))
-
-    blocks(PX - 2, end + 2, nyb, PY - 4, count_body)
+        return [(0, up.astype(jnp.float32), down.astype(jnp.float32))]
+
+    blocks(span(PX - 2, end + 2), PX - 2, nyb, PY - 4, count_body)
     start(z_c[0])
     recv(z_c[0])
 
-    def weight_body(p, r, k):
+    def weight_body(slot, p, r, k):
         c = rows(cnt, (), p, r)
         c = c + jnp.where(lane == 0, from_lower(0, k), 0.0)
         c = c + jnp.where(lane == cz - 1, from_upper(0, k), 0.0)
         cnt[p, pl.ds(r, 8), :] = c
         w = rows(ext_f, (0,), p, r) / c
+        packs = []
         for ch in range(chans):
             v = w if ch == 0 else w * rows(ext_f, (ch,), p, r)
             w0[ch, p, pl.ds(r, 8), :] = v
-            pack(1 + ch, k, v, v)
-
-    blocks(PX - 2, end + 2, nyb, PY - 4, weight_body)
-    start(z_c[1])
-    recv(z_c[1])
-
-    def shift_body(p, r, k):
+            packs.append((slot + ch, v, v))
+        return packs
+
+    def shift_body(slot, p, r, k):
         for ch in range(chans):
             v = rows(w0, (ch,), p, r)
             wp[ch, p, pl.ds(r, 8), :] = jnp.where(
-                lane == cz - 1, from_upper(1 + ch, k), pltpu.roll(v, cz - 1, 1))
+                lane == cz - 1, from_upper(slot + ch, k), pltpu.roll(v, cz - 1, 1))
             wm[ch, p, pl.ds(r, 8), :] = jnp.where(
-                lane == 0, from_lower(1 + ch, k), pltpu.roll(v, 1, 1))
-
-    blocks(PX - 2, end + 2, nyb, PY - 4, shift_body)
+                lane == 0, from_lower(slot + ch, k), pltpu.roll(v, 1, 1))
+        return []
 
     def average_body(p, r, k):
         e = rows(ext_e, (), p, r)
@@ -258,8 +277,7 @@
         inverse = 1.0 / whole(0)
         for ch in range(1, chans):
             avg[ch - 1, p, pl.ds(r, 8), :] = whole(ch) * inverse
-
-    blocks(PX - 1, end + 1, nyb, PY - 4, average_body)
+        return []
 
     def deposit_body(p, r, k):
         acc = [[None] * 3 for _ in range(fields)]
@@ -271,26 +289,57 @@
                 for i in range(3):
                     term = v if (ax, ay, i) == (0, 0, 0) else jnp.where(ms[i], v, 0.0)
                     acc[f][i] = term if acc[f][i] is None else acc[f][i] + term
+        packs = []
         for f in range(fields):
             here, up, down = acc[f]
             here = here + jnp.where(lane == 0, 0.0, pltpu.roll(up, 1, 1))
             here = here + jnp.where(lane == cz - 1, 0.0, pltpu.roll(down, cz - 1, 1))
             out_ref[0, f, p - PX, pl.ds(r - PY, 8), :] = here
-            pack(1 + chans + f, k, up, down)
-
-    blocks(PX, end, cy // 8, PY, deposit_body)
+            packs.append((1 + 2 * chans + f, up, down))
+        return packs
+
+    weight = lambda planes, slot: blocks(
+        planes, PX - 2, nyb, PY - 4, functools.partial(weight_body, slot))
+    shift = lambda planes, slot: blocks(
+        planes, PX - 2, nyb, PY - 4, functools.partial(shift_body, slot))
+    average = lambda planes: blocks(planes, PX - 1, nyb, PY - 4, average_body)
+    deposit = lambda planes: blocks(planes, PX, cy // 8, PY, deposit_body)
+
+    own, ghosts = span(PX, end), both_ends(PX - 2, end + 2)
+    weight(own, 1)
+    start(z_c[1])
+    recv(z_c[1])
+    shift(own, 1)
+    average(span(PX + 1, end - 1))
+    for c in (x_vf, x_u, c_f):
+        recv(c)
+    for side, has, at in x_sides:
+        @pl.when(has)
+        def _():
+            f0 = at - 2 if side == 0 else at
+            for ys, fr in ((0, PY - 2), (1, PY + cy)):
+                for c in range(chans):
+                    ext_f[c, f0:f0 + 2, fr:fr + 2, :] = cr_f[side, ys, c]
+    weight(ghosts, 1 + chans)
     start(z_c[2])
+    deposit(span(PX + 2, end - 2))
     recv(z_c[2])
+    shift(ghosts, 1 + chans)
+    average(both_ends(PX - 1, end + 1))
+    deposit(both_ends(PX, end))
+    start(z_c[3])
+    recv(z_c[3])
 
     def final_body(p, r, k):
         inverse = 1.0 / rows(cnt, (), p, r)
         for f in range(fields):
             v = out_ref[0, f, p - PX, pl.ds(r - PY, 8), :]
-            v = v + jnp.where(lane == 0, from_lower(1 + chans + f, k), 0.0)
-            v = v + jnp.where(lane == cz - 1, from_upper(1 + chans + f, k), 0.0)
+            v = v + jnp.where(lane == 0, from_lower(1 + 2 * chans + f, k), 0.0)
+            v = v + jnp.where(lane == cz - 1, from_upper(1 + 2 * chans + f, k), 0.0)
             out_ref[0, f, p - PX, pl.ds(r - PY, 8), :] = v * inverse
-
-    blocks(PX, end, cy // 8, PY, final_body)
+        return []
+
+    blocks(own, PX, cy // 8, PY, final_body)
     for c in everything:
         sent(c)
 
@@ -298,7 +347,7 @@
 def per_device(n, conserved, volume_fraction, cut_mask, merge_code):
     fields, cx, cy, cz = conserved.shape[1:]
     chans = fields + 1
-    ext = (cx + 6, cy + 16, cz)
+    ext = (cx + 7, cy + 24, cz)
     f32, i32 = jnp.float32, jnp.int32
     scratch = [
         pltpu.VMEM(ext, i32), pltpu.VMEM((chans,) + ext, f32), pltpu.VMEM(ext, f32),
@@ -308,8 +357,8 @@
         pltpu.VMEM((2, cx, 4, cz), i32), pltpu.VMEM((2, chans, cx, 2, cz), f32),
         pltpu.VMEM((2, cx, 4, cz), i32), pltpu.VMEM((2, chans, cx, 2, cz), f32),
         pltpu.VMEM((2, 2, 3, 4, cz), i32), pltpu.VMEM((2, 2, chans, 2, 2, cz), f32),
-        pltpu.VMEM((2, 1 + chans + fields, 8, cz), f32), pltpu.VMEM((2, 1 + chans + fields, 8, cz), f32),
-        pltpu.SemaphoreType.DMA((4,)), pltpu.SemaphoreType.DMA((20,)), pltpu.SemaphoreType.DMA((20,)),
+        pltpu.VMEM((2, 1 + 2 * chans + fields, 8, cz), f32), pltpu.VMEM((2, 1 + 2 * chans + fields, 8, cz), f32),
+        pltpu.SemaphoreType.DMA((4,)), pltpu.SemaphoreType.DMA((22,)), pltpu.SemaphoreType.DMA((22,)),
     ]
     return pl.pallas_call(
         functools.partial(kernel, n, (fields, cx, cy, cz)),
@@ -318,7 +367,7 @@
         out_specs=pl.BlockSpec(memory_space=pltpu.VMEM),
         scratch_shapes=scratch,
         compiler_params=pltpu.CompilerParams(
-            collective_id=0, has_side_effects=True, vmem_limit_bytes=48 * 1024 * 1024),
+            collective_id=0, has_side_effects=True, vmem_limit_bytes=60 * 1024 * 1024),
         name="redistribute",
     )(conserved, volume_fraction, cut_mask, merge_code)
 

time: 87.4 us -> 50.4 us (0.58)
  Pallas kernels: 81.1 us -> 46.9 us
  local copies, waits for them, and re-layouts: 5.22 us -> 2.52 us
    pallas_call x1, Pallas kernels: 81.1 us -> 46.9 us  [per_device(): pl.pallas_call(functools.partial(kernel, n, (fields, cx, cy, cz)), out_sh...]
    unnamed x9 -> x1, local copies, waits for them, and re-layouts: 5.22 us -> 2.52 us
where the time goes in v2:
time: 50.4 us; the launch traced here: 49.5 us
  Pallas kernels  46.9 us (93%)
  local copies, waits for them, and re-layouts  2.52 us (5%)
    pallas_call x1, Pallas kernels, per_device(): pl.pallas_call(functools.partial(kernel, n, (fields, cx, cy, cz)), out_sh...  46.9 us
    unnamed x1, local copies, waits for them, and re-layouts  2.52 us

profile of v2, /device:TPU:5, one launch (start us, length us, event | category | flops | bytes accessed | tf_op | source)
XLA Modules:
  0.0 49.5 jit_solution(118107194415708554)
XLA Ops:
  0.0 46.9 %redistribute.1 = f32[1,5,16,32,128]{4,3,2,1,0:T(8,128)} custom-call(f32[1,5,16,32,128]{4,3,2,1,0:T(8,128)} %u_ref.1, f32[1,16,32,128]{3,2,1,0:T(8,128)} %vf_ref.1, s32[1,16,32,128]{3,2,1,0:T(8,128)} %mask_ref.1, s32[1,16,32,128]{3,2,1,0:T(8,128)} %code_ref.1), custom_call_target="tpu_custom_call" | custom-call | tf_op jit(solution)/shard_map/redistribute/pallas_call | solution.py:363
  46.9 2.5 %copy.6 = f32[1,5,16,32,128]{4,3,2,1,0:T(8,128)} copy(f32[1,5,16,32,128]{4,3,2,1,0:T(8,128)} %redistribute.1) | data formatting | bytes 2621440
